TPU v7x, 32 devices: a whole 2x2x4 slice. The times are simulated.
32 devices in a mesh: blk: 32 (over z, y, x, core).
Axes of the slice: x: 2, y: 2, z: 4, core: 2. Of those that a mesh axis runs over, the one named last changes fastest.
Arguments:
- frames: float32 [128, 128, 1280], P('blk'), may hold values from -6 to 6
- widths: float32 [128], replicated, may hold values from 2 to 12
- kernel: float32 [3, 3], replicated, may hold values from -3 to 3
Outputs:
- filtered: float32 [128, 128, 1280], P(None, 'blk')
All inputs are finite; a program needn't handle non-finite values.
Results may differ from a plain program's by a relative error of at most 0.00007.
Values sent between devices are 32-bit elements; how exact they have to be, the bound alone decides.
A program may use at most 64 MiB of HBM per device.

v0:
```python
import jax
import jax.numpy as jnp
from jax import lax
from jax.sharding import PartitionSpec as P

BAND = 24


def temporal_matrix(widths, length):
    steps = jnp.arange(length, dtype=jnp.int32)
    offset = (steps[:, None] - steps[None, :]).astype(jnp.float32)
    inside = jnp.abs(offset) <= BAND
    spread = widths[:, None]
    weights = jnp.where(inside, jnp.exp(-offset * offset / (2.0 * spread * spread)), 0.0)
    return weights / jnp.sum(weights, axis=1, keepdims=True)


def stencil(padded, kernel):
    rows_out = padded.shape[1] - 2
    columns = padded.shape[2]
    widened = jnp.pad(padded, ((0, 0), (0, 0), (1, 1)))
    summed = jnp.zeros((padded.shape[0], rows_out, columns), jnp.float32)
    for row_off in range(3):
        for col_off in range(3):
            summed = (
                summed
                + kernel[row_off, col_off]
                * widened[:, row_off : row_off + rows_out, col_off : col_off + columns]
            )
    return summed


def local(frames, widths, kernel):
    weights = temporal_matrix(widths, widths.shape[0])
    local_filtered = stencil(jnp.pad(frames, ((0, 0), (1, 1), (0, 0))), kernel)
    return jnp.einsum(
        "ts,srw->trw",
        weights,
        lax.all_to_all(local_filtered, "blk", split_axis=1, concat_axis=0, tiled=True),
        precision=lax.Precision.HIGHEST,
    )


def solution(mesh):
    return jax.shard_map(
        local,
        mesh=mesh,
        in_specs=(P("blk", None, None), P(), P()),
        out_specs=P(None, "blk", None),
        check_vma=False,
    )
```

profile of v0, /device:TPU:0, one launch (start us, length us, event | category | flops | bytes accessed | tf_op | source)
XLA Modules:
  0.0 102.4 jit_solution(13410759657057529813)
XLA Ops:
  0.0 1.7 %fusion.13 = (f32[1,1]{1,0:T(1,128)}, f32[1,1]{1,0:T(1,128)}, f32[1,1]{1,0:T(1,128)}, f32[1,1]{1,0:T(1,128)}, f32[1,1]{1,0:T(1,128)}, /*index=5*/f32[1,1]{1,0:T(...) fusion(f32[3,3]{1,0:T(4,128)} %param.5), kind=kLoop, calls=%fused_computation.18 | loop fusion | bytes 72 | tf_op jit(solution)/shard_map/slice | solution.py:27
  1.7 3.4 %copy.6 = f32[4,128,1280]{2,0,1:T(4,128)S(1)} copy(f32[4,128,1280]{2,1,0:T(8,128)} %param.3) | data formatting | bytes 5242880 | tf_op args[0]
  5.1 0.0 copy-start
  5.1 0.5 pad.8
  5.6 1.3 %copy-done = f32[4,128,1280]{2,1,0:T(8,128)S(1)} copy-done((f32[4,128,1280]{2,1,0:T(8,128)S(1)}, f32[4,128,1280]{2,1,0:T(8,128)}, u32[]{:S(2)}) %copy-start) | copy-done | bytes 2621464
  6.9 17.9 %multiply_add_fusion = f32[4,128,1280]{2,0,1:T(4,128)} fusion(f32[4,130,1280]{2,0,1:T(4,128)S(1)} %pad.8, f32[]{:T(128)} %bitcast.9, f32[]{:T(128)} %bitcast.8, f32[]{:T(128)} %bitcast.7, f32[]{:T(128)} %bitcast.6, f32[]{:T(128)} %bitcast.5, f32[]{:T(128)} %bitcast.4, f32[]{:T(128)} %bitcast.3, f32[]{:T(128)} %bitcast.2, f32[]{:T(128)} %bitcast.1, ...), kind=kLoop, calls=%fused_computation.1 | loop fusion | flops 11141120 | bytes 13148196 | tf_op jit(solution)/shard_map/add | solution.py:26
  24.8 0.0 copy-start.1
  24.8 7.3 %all-to-all-start = ((f32[4,128,1280]{2,0,1:T(4,128)}), f32[4,128,1280]{2,0,1:T(4,128)S(1)}, u32[]{:S(2)}, u32[]{:S(2)}) async-start(f32[4,128,1280]{2,0,1:T(4,128)} %multiply_add_fusion), calls=%async_computation | async-start | bytes 5242880 | tf_op jit(solution)/shard_map/all_to_all | solution.py:39
  32.1 0.0 copy-done.1
  32.2 0.2 fusion.10
  32.3 59.9 %all-to-all-done = f32[4,128,1280]{2,0,1:T(4,128)S(1)} async-done(((f32[4,128,1280]{2,0,1:T(4,128)}), f32[4,128,1280]{2,0,1:T(4,128)S(1)}, u32[]{:S(2)}, u32[]{:S(2)}) %all-to-all-start) | async-done | bytes 2621472 | tf_op jit(solution)/shard_map/all_to_all | solution.py:39
  92.2 1.7 %copy.12 = f32[4,32,4,1280]{3,0,1,2:T(4,128)} copy(f32[4,32,4,1280]{3,0,2,1:T(4,128)S(1)} %bitcast.19) | data formatting | bytes 5242880 | tf_op jit(solution)/shard_map/all_to_all | solution.py:39
  93.9 2.8 %all_to_all.16 = f32[128,4,1280]{2,0,1:T(8,128)S(1)} reshape(f32[32,4,4,1280]{3,1,0,2:T(4,128)} %bitcast.20) | data formatting | bytes 5242880 | tf_op jit(solution)/shard_map/all_to_all | solution.py:39
  96.7 2.5 %fusion.5 = f32[128,4,1280]{2,0,1:T(8,128)S(1)} fusion(f32[128,4,1280]{2,0,1:T(8,128)S(1)} %all_to_all.16, f32[128]{0:T(128)S(1)} %fusion.10, f32[128]{0:T(128)S(1)} %multiply_multiply_fusion), kind=kOutput, calls=%fused_computation.9 | convolution fusion | flops 1006780416 | bytes 5243904 | tf_op jit(solution)/shard_map/ts,srw->trw/dot_general | solution.py:36
  99.2 3.2 %copy.9 = f32[128,4,1280]{2,1,0:T(4,128)} copy(f32[128,4,1280]{2,0,1:T(8,128)S(1)} %fusion.5) | data formatting | bytes 5242880 | tf_op jit(solution)/shard_map/ts,srw->trw/dot_general | solution.py:36
  (1 shorter events, 0.0 us)
Async XLA Ops:
  5.1 1.7 %copy-start = (f32[4,128,1280]{2,1,0:T(8,128)S(1)}, f32[4,128,1280]{2,1,0:T(8,128)}, u32[]{:S(2)}) copy-start(f32[4,128,1280]{2,1,0:T(8,128)} %param.3) | copy-start | bytes 7864324
  24.8 7.3 %copy-start.1 = (f32[128]{0:T(128)S(1)}, f32[128]{0:T(128)}, u32[]{:S(2)}) copy-start(f32[128]{0:T(128)} %param.4) | copy-start | bytes 1540
  24.8 67.4 %all-to-all-start = ((f32[4,128,1280]{2,0,1:T(4,128)}), f32[4,128,1280]{2,0,1:T(4,128)S(1)}, u32[]{:S(2)}, u32[]{:S(2)}) async-start(f32[4,128,1280]{2,0,1:T(4,128)} %multiply_add_fusion), calls=%async_computation | async-start | bytes 5242880 | tf_op jit(solution)/shard_map/all_to_all | solution.py:39
where the time goes:
time: 103 us; the launch traced here: 102 us
  waiting for transfers between devices  59.9 us (58%)
  other arithmetic  18.1 us (18%)
  local copies, waits for them, and re-layouts  14.5 us (14%)
  starting transfers between devices  7.33 us (7%)
  matrix products  2.49 us (2%)
    all_to_all x1, waiting for transfers between devices, local(): lax.all_to_all(local_filtered, 'blk', split_axis=1, concat_axis=0, tiled=...  59.9 us
    add x1, other arithmetic, stencil(): summed + kernel[row_off, col_off] * widened[:, row_off:row_off + rows_out...  17.9 us
    all_to_all x1, starting transfers between devices, local(): lax.all_to_all(local_filtered, 'blk', split_axis=1, concat_axis=0, tiled=...  7.33 us
    unnamed x5, local copies, waits for them, and re-layouts  4.7 us
    all_to_all x2, local copies, waits for them, and re-layouts, local(): lax.all_to_all(local_filtered, 'blk', split_axis=1, concat_axis=0, tiled=...  4.49 us
    dot_general x1, local copies, waits for them, and re-layouts, local(): jnp.einsum('ts,srw->trw', weights, lax.all_to_all(local_filtered, 'blk',...  3.18 us
    dot_general x1, matrix products, local(): jnp.einsum('ts,srw->trw', weights, lax.all_to_all(local_filtered, 'blk',...  2.49 us
  transfers between devices with their start and end apart: 1, of which 1 were waited for; matrix products, arithmetic and copies ran while one was open for 0% of the time, Pallas kernels for 0%

commit v1 on v0

v1 whole, which is shorter than its diff:
```python
import functools

import jax
import jax.numpy as jnp
from jax import lax
from jax.experimental import pallas as pl
from jax.experimental.pallas import tpu as pltpu
from jax.sharding import PartitionSpec as P

BAND = 24
MESH = pl.DeviceIdType.MESH


def exchange_kernel(
    n,
    frames_ref,
    widths_ref,
    kernel_ref,
    out_ref,
    held,
    outgoing,
    incoming,
    mixing,
    in_sem,
    send_sem,
    recv_sem,
):
    per_device, height, columns = frames_ref.shape
    chunks, _, rows_block, chunk = outgoing.shape
    rows = rows_block // per_device
    group = 8 // rows
    groups = n // group
    length = widths_ref.shape[1]
    me = lax.axis_index("blk")
    half = max(groups // 2, 1)

    load = pltpu.make_async_copy(frames_ref, held.at[:, pl.ds(8, height), :], in_sem)
    load.start()
    barrier = pltpu.get_barrier_semaphore()

    @pl.loop(1, n)
    def _(step):
        pl.semaphore_signal(
            barrier, inc=1, device_id=(lax.rem(me + step, n),), device_id_type=MESH
        )

    edge = jnp.zeros((per_device, 8, columns), jnp.float32)
    held[:, pl.ds(0, 8), :] = edge
    held[:, pl.ds(height + 8, 8), :] = edge
    load.wait()

    own = me // group
    own_half = own // half

    def group_at(step):
        far = step < half
        base = jnp.where(far, (1 - own_half) * half, own_half * half)
        return base + lax.rem(own + step + 1, half)

    column = lax.broadcasted_iota(jnp.int32, (8, columns), 1)

    def filter_group(at):
        for frame in range(per_device):
            tall = held[frame, pl.ds(pl.multiple_of(at * 8, 8), 24), :]
            taps = [tall[7:15], tall[8:16], tall[9:17]]
            mixed = [
                kernel_ref[0, col] * taps[0]
                + kernel_ref[1, col] * taps[1]
                + kernel_ref[2, col] * taps[2]
                for col in range(3)
            ]
            left = jnp.where(column == 0, 0.0, pltpu.roll(mixed[0], 1, 1))
            right = jnp.where(
                column == columns - 1, 0.0, pltpu.roll(mixed[2], columns - 1, 1)
            )
            value = left + mixed[1] + right
            for member in range(group):
                for k in range(chunks):
                    outgoing[
                        k, at * group + member, pl.ds(frame * rows, rows), :
                    ] = value[
                        member * rows : (member + 1) * rows,
                        k * chunk : (k + 1) * chunk,
                    ]

    def send(k, target):
        pltpu.make_async_remote_copy(
            src_ref=outgoing.at[k, target],
            dst_ref=incoming.at[k, me],
            send_sem=send_sem.at[k],
            recv_sem=recv_sem.at[k],
            device_id=(target,),
            device_id_type=MESH,
        ).start()

    def send_own_group(k):
        for other in range(1, group):
            send(k, own * group + lax.rem(me + other, group))
        pltpu.make_async_copy(
            outgoing.at[k, me], incoming.at[k, me], recv_sem.at[k]
        ).start()

    filter_group(group_at(0))
    pl.semaphore_wait(barrier, n - 1)

    @pl.loop(0, groups - 1)
    def _(step):
        at = group_at(step)
        filter_group(group_at(step + 1))
        for member in range(group):
            send(0, at * group + member)

    send_own_group(0)

    @pl.loop(1, chunks)
    def _(k):
        @pl.loop(0, groups - 1)
        def _(step):
            at = group_at(step)
            for member in range(group):
                send(k, at * group + member)

        send_own_group(k)

    total = length * rows
    target_at = lax.broadcasted_iota(jnp.int32, (total, length), 0) // rows
    lane = lax.broadcasted_iota(jnp.int32, (total, length), 1)
    spread = jnp.sum(
        jnp.where(target_at == lane, widths_ref[...], 0.0), axis=1, keepdims=True
    )
    row_at = lax.broadcasted_iota(jnp.int32, (total, total), 0)
    col_at = lax.broadcasted_iota(jnp.int32, (total, total), 1)
    apart = row_at // rows - col_at // rows
    inside = (jnp.abs(apart) <= BAND) & (row_at % rows == col_at % rows)
    offset = apart.astype(jnp.float32)
    weights = jnp.where(
        inside, jnp.exp(-offset * offset / (2.0 * spread * spread)), 0.0
    )
    mixing[...] = weights / jnp.sum(weights, axis=1, keepdims=True)

    @pl.loop(0, chunks)
    def _(k):
        pltpu.make_async_copy(incoming.at[k], incoming.at[k], recv_sem.at[k]).wait()
        if rows_block % 8 == 0:
            block = incoming[k].reshape(total, chunk)
        else:
            block = jnp.concatenate([incoming[k, s] for s in range(n)], axis=0)
        out_ref[:, pl.ds(pl.multiple_of(k * chunk, 128), chunk)] = jnp.dot(
            mixing[...],
            block,
            precision=lax.Precision.HIGHEST,
            preferred_element_type=jnp.float32,
        )

    @pl.loop(0, chunks)
    def _(k):
        sent = outgoing.at[k, pl.ds(0, n - 1)]
        pltpu.make_async_copy(sent, sent, send_sem.at[k]).wait()


def local(n, frames, widths, kernel):
    per_device, height, columns = frames.shape
    length = widths.shape[0]
    rows = height // n
    chunk = 256 if columns % 256 == 0 else 128
    chunks = columns // chunk
    vmem = pl.BlockSpec(memory_space=pltpu.VMEM)
    mixed = pl.pallas_call(
        functools.partial(exchange_kernel, n),
        out_shape=jax.ShapeDtypeStruct((length * rows, columns), jnp.float32),
        in_specs=[
            pl.BlockSpec(memory_space=pl.ANY),
            vmem,
            pl.BlockSpec(memory_space=pltpu.SMEM),
        ],
        out_specs=vmem,
        scratch_shapes=[
            pltpu.VMEM((per_device, height + 16, columns), jnp.float32),
            pltpu.VMEM((chunks, n, per_device * rows, chunk), jnp.float32),
            pltpu.VMEM((chunks, n, per_device * rows, chunk), jnp.float32),
            pltpu.VMEM((length * rows, length * rows), jnp.float32),
            pltpu.SemaphoreType.DMA,
            pltpu.SemaphoreType.DMA((chunks,)),
            pltpu.SemaphoreType.DMA((chunks,)),
        ],
        compiler_params=pltpu.CompilerParams(
            collective_id=0,
            has_side_effects=True,
            vmem_limit_bytes=36 * 1024 * 1024,
        ),
    )(frames, widths.reshape(1, length), kernel)
    return mixed.reshape(length, rows, columns)


def solution(mesh):
    return jax.shard_map(
        functools.partial(local, mesh.shape["blk"]),
        mesh=mesh,
        in_specs=(P("blk", None, None), P(), P()),
        out_specs=P(None, "blk", None),
        check_vma=False,
    )
```

time: 103 us -> 72.1 us (0.70)
  Pallas kernels: 0 us -> 67 us
  waiting for transfers between devices: 59.9 us -> 0 us
  other arithmetic: 18.1 us -> 0 us
  local copies, waits for them, and re-layouts: 14.5 us -> 4.97 us
  starting transfers between devices: 7.33 us -> 0 us
  matrix products: 2.49 us -> 0 us
    pallas_call x0 -> x1, Pallas kernels: none -> 67 us  [local(): pl.pallas_call(functools.partial(exchange_kernel, n), out_shape=jax.Shape...]
    all_to_all x1 -> x0, waiting for transfers between devices: 59.9 us -> none  [local(): lax.all_to_all(local_filtered, 'blk', split_axis=1, concat_axis=0, tiled=...]
    add x1 -> x0, other arithmetic: 17.9 us -> none  [stencil(): summed + kernel[row_off, col_off] * widened[:, row_off:row_off + rows_out...]
    all_to_all x1 -> x0, starting transfers between devices: 7.33 us -> none  [local(): lax.all_to_all(local_filtered, 'blk', split_axis=1, concat_axis=0, tiled=...]
    all_to_all x2 -> x0, local copies, waits for them, and re-layouts: 4.49 us -> none  [local(): lax.all_to_all(local_filtered, 'blk', split_axis=1, concat_axis=0, tiled=...]
    dot_general x1 -> x0, local copies, waits for them, and re-layouts: 3.18 us -> none  [local(): jnp.einsum('ts,srw->trw', weights, lax.all_to_all(local_filtered, 'blk',...]
    dot_general x1 -> x0, matrix products: 2.49 us -> none  [local(): jnp.einsum('ts,srw->trw', weights, lax.all_to_all(local_filtered, 'blk',...]
    reshape x0 -> x1, local copies, waits for them, and re-layouts: none -> 1.89 us  [local(): return mixed.reshape(length, rows, columns)]
  transfers between devices with their start and end apart: 1 -> 0, of which waited for: 1 -> 0; matrix products, arithmetic and copies ran while one was open for 0% -> 0% of each run, Pallas kernels for 0% -> 0%
where the time goes in v1:
time: 72.1 us; the launch traced here: 72 us
  Pallas kernels  67 us (93%)
  local copies, waits for them, and re-layouts  4.97 us (7%)
    pallas_call x1, Pallas kernels, local(): pl.pallas_call(functools.partial(exchange_kernel, n), out_shape=jax.Shape...  67 us
    unnamed x6, local copies, waits for them, and re-layouts  3.08 us
    reshape x1, local copies, waits for them, and re-layouts, local(): return mixed.reshape(length, rows, columns)  1.89 us

profile of v1, /device:TPU:0, one launch (start us, length us, event | category | flops | bytes accessed | tf_op | source)
XLA Modules:
  0.0 72.0 jit_solution(16525641588855122946)
XLA Ops:
  0.0 0.0 copy-start
  0.0 1.7 %copy-done = f32[4,128,1280]{2,1,0:T(8,128)S(1)} copy-done((f32[4,128,1280]{2,1,0:T(8,128)S(1)}, f32[4,128,1280]{2,1,0:T(8,128)}, u32[]{:S(2)}) %copy-start) | copy-done | bytes 2621464
  1.7 0.0 copy-start.1
  1.7 0.7 copy-done.1
  2.4 0.0 copy-start.2
  2.4 0.7 copy-done.2
  3.1 67.0 %shard_map.37 = f32[512,1280]{1,0:T(8,128)S(1)} custom-call(f32[4,128,1280]{2,1,0:T(8,128)S(1)} %copy-done, f32[1,128]{1,0:T(1,128)S(1)} %bitcast.1, f32[3,3]{1,0:T(4,128)S(1)} %copy-done.1), custom_call_target="tpu_custom_call" | custom-call | tf_op jit(solution)/shard_map/pallas_call | solution.py:168
  70.1 1.9 %reshape.7 = f32[128,4,1280]{2,1,0:T(4,128)} reshape(f32[512,1280]{1,0:T(8,128)S(1)} %shard_map.37) | data formatting | bytes 5242880 | tf_op jit(solution)/shard_map/reshape | solution.py:192
Async XLA Ops:
  0.0 1.7 %copy-start = (f32[4,128,1280]{2,1,0:T(8,128)S(1)}, f32[4,128,1280]{2,1,0:T(8,128)}, u32[]{:S(2)}) copy-start(f32[4,128,1280]{2,1,0:T(8,128)} %frames_ref.1) | copy-start | bytes 7864324
  1.7 0.7 copy-start.1
  2.4 0.7 copy-start.2

commit v2 on v1

--- a/solution.py
+++ b/solution.py
@@ -14,16 +14,19 @@
 def exchange_kernel(
     n,
     frames_ref,
-    widths_ref,
-    kernel_ref,
+    widths_hbm,
+    kernel_hbm,
     out_ref,
     held,
     outgoing,
     incoming,
     mixing,
+    widths_ref,
+    kernel_ref,
     in_sem,
     send_sem,
     recv_sem,
+    relay_sem,
 ):
     per_device, height, columns = frames_ref.shape
     chunks, _, rows_block, chunk = outgoing.shape
@@ -32,30 +35,50 @@
     groups = n // group
     length = widths_ref.shape[1]
     me = lax.axis_index("blk")
-    half = max(groups // 2, 1)
-
-    load = pltpu.make_async_copy(frames_ref, held.at[:, pl.ds(8, height), :], in_sem)
-    load.start()
+    quarter = n // 4
+    mine = me // quarter
+    place = me - mine * quarter
+    mirror = 3 - mine
+    beside = mine + 1 - 2 * lax.rem(mine, 2)
+    across = mirror + 1 - 2 * lax.rem(mirror, 2)
+    partner = beside * quarter + place
+    opposite = mirror * quarter + place
+
+    loads = [
+        pltpu.make_async_copy(
+            frames_ref, held.at[:, pl.ds(8, height), :], in_sem.at[0]
+        ),
+        pltpu.make_async_copy(kernel_hbm, kernel_ref, in_sem.at[1]),
+        pltpu.make_async_copy(widths_hbm, widths_ref, in_sem.at[2]),
+    ]
+    for load in loads:
+        load.start()
+
+    def signal(semaphore, target):
+        pl.semaphore_signal(
+            semaphore, inc=1, device_id=(target,), device_id_type=MESH
+        )
+
     barrier = pltpu.get_barrier_semaphore()
 
-    @pl.loop(1, n)
+    @pl.loop(0, quarter)
     def _(step):
-        pl.semaphore_signal(
-            barrier, inc=1, device_id=(lax.rem(me + step, n),), device_id_type=MESH
-        )
+        signal(barrier, mirror * quarter + lax.rem(place + step, quarter))
+
+    signal(barrier, partner)
 
     edge = jnp.zeros((per_device, 8, columns), jnp.float32)
     held[:, pl.ds(0, 8), :] = edge
     held[:, pl.ds(height + 8, 8), :] = edge
-    load.wait()
-
+    for load in loads:
+        load.wait()
+
+    part = quarter // group
     own = me // group
-    own_half = own // half
-
-    def group_at(step):
-        far = step < half
-        base = jnp.where(far, (1 - own_half) * half, own_half * half)
-        return base + lax.rem(own + step + 1, half)
+    seat = place // group
+
+    def group_at(which, step):
+        return which * part + lax.rem(seat + step, part)
 
     column = lax.broadcasted_iota(jnp.int32, (8, columns), 1)
 
@@ -100,27 +123,50 @@
             outgoing.at[k, me], incoming.at[k, me], recv_sem.at[k]
         ).start()
 
-    filter_group(group_at(0))
-    pl.semaphore_wait(barrier, n - 1)
-
-    @pl.loop(0, groups - 1)
-    def _(step):
-        at = group_at(step)
-        filter_group(group_at(step + 1))
-        for member in range(group):
-            send(0, at * group + member)
-
-    send_own_group(0)
-
-    @pl.loop(1, chunks)
-    def _(k):
-        @pl.loop(0, groups - 1)
+    def filter_quarter(which):
+        @pl.loop(0, part)
         def _(step):
-            at = group_at(step)
+            filter_group(group_at(which, step))
+
+    def send_quarter(which, k):
+        @pl.loop(0, part)
+        def _(step):
+            at = group_at(which, step)
             for member in range(group):
                 send(k, at * group + member)
 
+    def send_near(k):
+        @pl.loop(1, part)
+        def _(step):
+            at = group_at(mine, step)
+            for member in range(group):
+                send(k, at * group + member)
+
         send_own_group(k)
+
+    filter_quarter(mirror)
+    pl.semaphore_wait(barrier, quarter + 1)
+    signal(relay_sem.at[0], partner)
+
+    @pl.loop(0, chunks)
+    def _(k):
+        send_quarter(mirror, k)
+
+    filter_quarter(across)
+    pl.semaphore_wait(relay_sem.at[0], 1)
+    signal(relay_sem.at[1], opposite)
+    send_quarter(across, 0)
+    filter_quarter(beside)
+    filter_quarter(mine)
+    pl.semaphore_wait(relay_sem.at[1], 1)
+    send_quarter(beside, 0)
+    send_near(0)
+
+    @pl.loop(1, chunks)
+    def _(k):
+        send_quarter(across, k)
+        send_quarter(beside, k)
+        send_near(k)
 
     total = length * rows
     target_at = lax.broadcasted_iota(jnp.int32, (total, length), 0) // rows
@@ -168,20 +214,19 @@
     mixed = pl.pallas_call(
         functools.partial(exchange_kernel, n),
         out_shape=jax.ShapeDtypeStruct((length * rows, columns), jnp.float32),
-        in_specs=[
-            pl.BlockSpec(memory_space=pl.ANY),
-            vmem,
-            pl.BlockSpec(memory_space=pltpu.SMEM),
-        ],
+        in_specs=[pl.BlockSpec(memory_space=pltpu.HBM)] * 3,
         out_specs=vmem,
         scratch_shapes=[
             pltpu.VMEM((per_device, height + 16, columns), jnp.float32),
             pltpu.VMEM((chunks, n, per_device * rows, chunk), jnp.float32),
             pltpu.VMEM((chunks, n, per_device * rows, chunk), jnp.float32),
             pltpu.VMEM((length * rows, length * rows), jnp.float32),
-            pltpu.SemaphoreType.DMA,
+            pltpu.VMEM((1, length), jnp.float32),
+            pltpu.SMEM((3, 3), jnp.float32),
+            pltpu.SemaphoreType.DMA((3,)),
             pltpu.SemaphoreType.DMA((chunks,)),
             pltpu.SemaphoreType.DMA((chunks,)),
+            pltpu.SemaphoreType.REGULAR((2,)),
         ],
         compiler_params=pltpu.CompilerParams(
             collective_id=0,

time: 72.1 us -> 70.2 us (0.974)
  Pallas kernels: 67 us -> 65.1 us
    pallas_call x1, Pallas kernels: 67 us -> 65.1 us  [local(): pl.pallas_call(functools.partial(exchange_kernel, n), out_shape=jax.Shape...]
where the time goes in v2:
time: 70.2 us; the launch traced here: 70 us
  Pallas kernels  65.1 us (93%)
  local copies, waits for them, and re-layouts  4.97 us (7%)
    pallas_call x1, Pallas kernels, local(): pl.pallas_call(functools.partial(exchange_kernel, n), out_shape=jax.Shape...  65.1 us
    unnamed x6, local copies, waits for them, and re-layouts  3.08 us
    reshape x1, local copies, waits for them, and re-layouts, local(): return mixed.reshape(length, rows, columns)  1.89 us

profile of v2, /device:TPU:0, one launch (start us, length us, event | category | flops | bytes accessed | tf_op | source)
XLA Modules:
  0.0 70.0 jit_solution(14686949544392897137)
XLA Ops:
  0.0 0.0 copy-start
  0.0 1.7 %copy-done = f32[4,128,1280]{2,1,0:T(8,128)S(1)} copy-done((f32[4,128,1280]{2,1,0:T(8,128)S(1)}, f32[4,128,1280]{2,1,0:T(8,128)}, u32[]{:S(2)}) %copy-start) | copy-done | bytes 2621464
  1.7 0.0 copy-start.1
  1.7 0.7 copy-done.1
  2.4 0.0 copy-start.2
  2.4 0.7 copy-done.2
  3.1 65.1 %shard_map.37 = f32[512,1280]{1,0:T(8,128)S(1)} custom-call(f32[4,128,1280]{2,1,0:T(8,128)S(1)} %copy-done, f32[1,128]{1,0:T(1,128)S(1)} %bitcast.1, f32[3,3]{1,0:T(4,128)S(1)} %copy-done.1), custom_call_target="tpu_custom_call" | custom-call | tf_op jit(solution)/shard_map/pallas_call | solution.py:214
  68.2 1.9 %reshape.7 = f32[128,4,1280]{2,1,0:T(4,128)} reshape(f32[512,1280]{1,0:T(8,128)S(1)} %shard_map.37) | data formatting | bytes 5242880 | tf_op jit(solution)/shard_map/reshape | solution.py:237
Async XLA Ops:
  0.0 1.7 %copy-start = (f32[4,128,1280]{2,1,0:T(8,128)S(1)}, f32[4,128,1280]{2,1,0:T(8,128)}, u32[]{:S(2)}) copy-start(f32[4,128,1280]{2,1,0:T(8,128)} %frames_ref.1) | copy-start | bytes 7864324
  1.7 0.7 copy-start.1
  2.4 0.7 copy-start.2

commit v3 on v2

--- a/solution.py
+++ b/solution.py
@@ -18,6 +18,7 @@
     kernel_hbm,
     out_ref,
     held,
+    window,
     outgoing,
     incoming,
     mixing,
@@ -44,15 +45,30 @@
     partner = beside * quarter + place
     opposite = mirror * quarter + place
 
-    loads = [
-        pltpu.make_async_copy(
-            frames_ref, held.at[:, pl.ds(8, height), :], in_sem.at[0]
-        ),
+    strip = height // 4
+    first = mirror * strip
+    above = jnp.where(mirror == 0, 0, first - 8)
+    below = jnp.where(mirror == 3, height - 8, first + strip)
+
+    def load(source, rows_in, target, at, semaphore):
+        return pltpu.make_async_copy(
+            frames_ref.at[:, pl.ds(pl.multiple_of(source, 8), rows_in), :],
+            target.at[:, pl.ds(at, rows_in), :],
+            semaphore,
+        )
+
+    early = [
         pltpu.make_async_copy(kernel_hbm, kernel_ref, in_sem.at[1]),
+        load(first, strip, window, 8, in_sem.at[3]),
+        load(above, 8, window, 0, in_sem.at[4]),
+        load(below, 8, window, strip + 8, in_sem.at[5]),
+    ]
+    late = [
+        load(0, height, held, 8, in_sem.at[0]),
         pltpu.make_async_copy(widths_hbm, widths_ref, in_sem.at[2]),
     ]
-    for load in loads:
-        load.start()
+    for copy in early:
+        copy.start()
 
     def signal(semaphore, target):
         pl.semaphore_signal(
@@ -70,8 +86,18 @@
     edge = jnp.zeros((per_device, 8, columns), jnp.float32)
     held[:, pl.ds(0, 8), :] = edge
     held[:, pl.ds(height + 8, 8), :] = edge
-    for load in loads:
-        load.wait()
+    for copy in early:
+        copy.wait()
+    for copy in late:
+        copy.start()
+
+    @pl.when(mirror == 0)
+    def _():
+        window[:, pl.ds(0, 8), :] = edge
+
+    @pl.when(mirror == 3)
+    def _():
+        window[:, pl.ds(strip + 8, 8), :] = edge
 
     part = quarter // group
     own = me // group
@@ -82,9 +108,9 @@
 
     column = lax.broadcasted_iota(jnp.int32, (8, columns), 1)
 
-    def filter_group(at):
+    def filter_group(at, source, base):
         for frame in range(per_device):
-            tall = held[frame, pl.ds(pl.multiple_of(at * 8, 8), 24), :]
+            tall = source[frame, pl.ds(pl.multiple_of((at - base) * 8, 8), 24), :]
             taps = [tall[7:15], tall[8:16], tall[9:17]]
             mixed = [
                 kernel_ref[0, col] * taps[0]
@@ -126,7 +152,7 @@
     def filter_quarter(which):
         @pl.loop(0, part)
         def _(step):
-            filter_group(group_at(which, step))
+            filter_group(group_at(which, step), held, 0)
 
     def send_quarter(which, k):
         @pl.loop(0, part)
@@ -144,14 +170,29 @@
 
         send_own_group(k)
 
-    filter_quarter(mirror)
+    def filter_early(step):
+        filter_group(group_at(mirror, step), window, mirror * part)
+
+    def send_early(step):
+        at = group_at(mirror, step)
+
+        @pl.loop(0, chunks)
+        def _(k):
+            for member in range(group):
+                send(k, at * group + member)
+
+    filter_early(0)
     pl.semaphore_wait(barrier, quarter + 1)
     signal(relay_sem.at[0], partner)
 
-    @pl.loop(0, chunks)
-    def _(k):
-        send_quarter(mirror, k)
-
+    @pl.loop(0, part - 1)
+    def _(step):
+        send_early(step)
+        filter_early(step + 1)
+
+    send_early(part - 1)
+    for copy in late:
+        copy.wait()
     filter_quarter(across)
     pl.semaphore_wait(relay_sem.at[0], 1)
     signal(relay_sem.at[1], opposite)
@@ -218,12 +259,13 @@
         out_specs=vmem,
         scratch_shapes=[
             pltpu.VMEM((per_device, height + 16, columns), jnp.float32),
+            pltpu.VMEM((per_device, height // 4 + 16, columns), jnp.float32),
             pltpu.VMEM((chunks, n, per_device * rows, chunk), jnp.float32),
             pltpu.VMEM((chunks, n, per_device * rows, chunk), jnp.float32),
             pltpu.VMEM((length * rows, length * rows), jnp.float32),
             pltpu.VMEM((1, length), jnp.float32),
             pltpu.SMEM((3, 3), jnp.float32),
-            pltpu.SemaphoreType.DMA((3,)),
+            pltpu.SemaphoreType.DMA((6,)),
             pltpu.SemaphoreType.DMA((chunks,)),
             pltpu.SemaphoreType.DMA((chunks,)),
             pltpu.SemaphoreType.REGULAR((2,)),
@@ -231,7 +273,7 @@
         compiler_params=pltpu.CompilerParams(
             collective_id=0,
             has_side_effects=True,
-            vmem_limit_bytes=36 * 1024 * 1024,
+            vmem_limit_bytes=50 * 1024 * 1024,
         ),
     )(frames, widths.reshape(1, length), kernel)
     return mixed.reshape(length, rows, columns)

time: 70.2 us -> 68.5 us (0.976)
  local copies, waits for them, and re-layouts: 4.97 us -> 3.23 us
    unnamed x6 -> x4, local copies, waits for them, and re-layouts: 3.08 us -> 1.34 us
where the time goes in v3:
time: 68.5 us; the launch traced here: 68.3 us
  Pallas kernels  65.1 us (95%)
  local copies, waits for them, and re-layouts  3.23 us (5%)
    pallas_call x1, Pallas kernels, local(): pl.pallas_call(functools.partial(exchange_kernel, n), out_shape=jax.Shape...  65.1 us
    reshape x1, local copies, waits for them, and re-layouts, local(): return mixed.reshape(length, rows, columns)  1.89 us

profile of v3, /device:TPU:0, one launch (start us, length us, event | category | flops | bytes accessed | tf_op | source)
XLA Modules:
  0.0 68.3 jit_solution(7143708162742517229)
XLA Ops:
  0.0 0.0 copy-start
  0.0 0.7 copy-done
  0.7 0.0 copy-start.1
  0.7 0.7 copy-done.1
  1.3 65.1 %shard_map.37 = f32[512,1280]{1,0:T(8,128)S(1)} custom-call(f32[4,128,1280]{2,1,0:T(8,128)} %frames_ref.1, f32[1,128]{1,0:T(1,128)S(1)} %bitcast.1, f32[3,3]{1,0:T(4,128)S(1)} %copy-done), custom_call_target="tpu_custom_call" | custom-call | tf_op jit(solution)/shard_map/pallas_call | solution.py:255
  66.4 1.9 %reshape.7 = f32[128,4,1280]{2,1,0:T(4,128)} reshape(f32[512,1280]{1,0:T(8,128)S(1)} %shard_map.37) | data formatting | bytes 5242880 | tf_op jit(solution)/shard_map/reshape | solution.py:279
Async XLA Ops:
  0.0 0.7 copy-start
  0.7 0.7 copy-start.1
